TPU v7x, 32 devices: a whole 2x2x4 slice. The times are simulated.
32 devices in a mesh: elem: 8 (over z, core), lev: 4 (over y, x).
Axes of the slice: x: 2, y: 2, z: 4, core: 2. Of those that a mesh axis runs over, the one named last changes fastest.
Arguments:
- tracers: float32 [512, 16, 640], P('elem', 'lev'), may hold values from 0.1 to 120, as said below
- ref_index: int32 [512, 16], P('elem'), may hold values from 0 to 63
- requests: int32 [8, 2, 16], P('elem'), may hold values from -1 to 63, as said below
- source: int32 [512], P('elem'), may hold values from 0 to 95, as said below
- target_mean: float32 [40], replicated, may hold values from 0.5 to 5
Outputs:
- transported: float32 [512, 16, 640], P('elem', 'lev')
Inputs may be any that keep to these rules, and one draw needn't show every extreme that they name: Row 0 of requests[d] holds distinct element indices of block d - 1 (wrapping), row 1 of block d + 1; the valid entries come first and the rest are -1; every row holds 1 to 16 valid entries and some row holds exactly 16. `source`: every slot names an own element (below 64) or a valid entry of the block's requests: 64 + k for row 0, 80 + k for row 1. `tracers`: all entries are positive.
All inputs are finite; a program needn't handle non-finite values.
Results may differ from a plain program's by a relative error of at most 0.0003.
Values sent between devices are 32-bit elements; how exact they have to be, the bound alone decides.
A program may use at most 64 MiB of HBM per device.

v0:
```python
import math

import jax
import jax.numpy as jnp
from jax import lax
from jax.sharding import PartitionSpec as P

NPTS = 16
REFS = 64


def with_halo(cells, sides, width):
    for axis, dim in sides:
        count = lax.axis_size(axis)
        head = lax.slice_in_dim(cells, 0, width, axis=dim)
        tail = lax.slice_in_dim(cells, cells.shape[dim] - width, cells.shape[dim], axis=dim)
        cells = jnp.concatenate(
            [
                lax.ppermute(tail, axis, [(i, (i + 1) % count) for i in range(count)]),
                cells,
                lax.ppermute(head, axis, [((i + 1) % count, i) for i in range(count)]),
            ],
            axis=dim,
        )
    return cells


def lagrange_table():
    side = math.isqrt(REFS)
    gll_nodes = [-1.0, -math.sqrt(0.2), math.sqrt(0.2), 1.0]
    points = -1.0 + 2.0 * jnp.arange(side, dtype=jnp.float32) / (side - 1)
    columns = []
    for which in range(4):
        basis = jnp.ones((side,), jnp.float32)
        for other in range(4):
            if other != which:
                basis = basis * (points - gll_nodes[other]) / (gll_nodes[which] - gll_nodes[other])
        columns.append(basis)
    one_dim = jnp.stack(columns, axis=1)
    return (one_dim[:, None, :, None] * one_dim[None, :, None, :]).reshape(side * side, 16)


def quadrature():
    edge = jnp.array([1.0 / 6.0, 5.0 / 6.0, 5.0 / 6.0, 1.0 / 6.0], jnp.float32)
    return (edge[:, None] * edge[None, :]).reshape(16)


def interpolate(source_rows, ref_index):
    elem_count, levels, width = source_rows.shape
    onehot = (ref_index[:, :, None] == jnp.arange(REFS, dtype=jnp.int32)[None, None, :]).astype(
        jnp.float32
    )
    matrix = jnp.einsum("epr,rn->epn", onehot, lagrange_table(), precision=lax.Precision.HIGHEST)
    values = source_rows.reshape(elem_count, levels * (width // 16), 16)
    result = jnp.einsum("epn,ecn->ecp", matrix, values, precision=lax.Precision.HIGHEST)
    lowest = jnp.min(values, axis=2, keepdims=True)
    highest = jnp.max(values, axis=2, keepdims=True)
    result = jnp.minimum(jnp.maximum(result, lowest), highest)
    return result.reshape(elem_count, levels, width)


def per_device(tracers, ref_index, requests, source, target_mean):
    elem_count, levels, width = tracers.shape
    beside_all = with_halo(tracers, (("elem", 0),), elem_count)
    own_pos = jnp.arange(elem_count, 2 * elem_count, dtype=jnp.int32)
    left_pos = jnp.maximum(requests[0, 0], 0)
    right_pos = 2 * elem_count + jnp.maximum(requests[0, 1], 0)
    slot_pos = jnp.concatenate([own_pos, left_pos, right_pos])
    source_rows = beside_all[slot_pos[source]]
    clipped = interpolate(source_rows, ref_index)
    tracer_count = width // NPTS
    shaped = clipped.reshape(elem_count, levels, tracer_count, NPTS)
    local_mass = jnp.einsum("eltn,n->t", shaped, quadrature(), precision=lax.Precision.HIGHEST)
    column_mass = lax.psum(local_mass, "lev")
    global_mass = lax.psum(column_mass, "elem")
    whole_weight = 4.0 * elem_count * lax.axis_size("elem") * levels * lax.axis_size("lev")
    factor = target_mean * whole_weight / global_mass
    return (shaped * factor[None, None, :, None]).reshape(elem_count, levels, width)


def solution(mesh):
    placed = (P("elem", "lev", None), P("elem", None), P("elem", None, None), P("elem"), P())
    return jax.shard_map(
        per_device, mesh=mesh, in_specs=placed, out_specs=P("elem", "lev", None), check_vma=False
    )
```

profile of v0, /device:TPU:0, one launch (start us, length us, event | category | flops | bytes accessed | tf_op | source)
XLA Modules:
  0.0 54.3 jit_solution(1006085163537011619)
XLA Ops:
  0.0 4.5 %collective-permute-start.1 = (f32[64,4,640]{2,1,0:T(4,128)}, f32[64,4,640]{2,1,0:T(4,128)S(1)}, u32[]{:S(2)}, u32[]{:S(2)}) collective-permute-start(f32[64,4,640]{2,1,0:T(4,128)} %param.6), channel_id=1, source_target_pairs={{4,0},{8,4},{12,8},{16,12},{20,16},{24,20},{28,24},{0,28},{5,1},{9... | collective-permute-start | bytes 1966088 | tf_op jit(solution)/shard_map/ppermute | solution.py:21
  4.6 0.8 %maximum_bitcast_fusion = (s32[16]{0:T(128)S(1)}, s32[16]{0:T(128)S(1)}) fusion(s32[1,2,16]{2,1,0:T(2,128)} %param.8), kind=kLoop, calls=%fused_computation.29 | loop fusion | flops 48 | bytes 256 | tf_op jit(solution)/shard_map/max | solution.py:66
  5.4 0.1 reshape.146
  5.5 1.5 %fusion.1 = f32[64,16,16]{0,2,1:T(8,128)S(1)} fusion(f32[64,16,1]{0,1,2:T(8,128)S(1)} %reshape.146, s32[64,16]{0,1:T(8,128)} %param.7), kind=kOutput, calls=%fused_computation.8 | convolution fusion | flops 12648448 | bytes 73728 | tf_op jit(solution)/shard_map/epr,rn->epn/dot_general | solution.py:53
  7.0 1.0 %copy.23 = f32[64,16,16]{2,1,0:T(8,128)} copy(f32[64,16,16]{0,2,1:T(8,128)S(1)} %fusion.1) | data formatting | bytes 131072 | tf_op jit(solution)/shard_map/epr,rn->epn/dot_general | solution.py:53
  8.0 0.8 %broadcast_multiply_fusion.1 = f32[4,4]{1,0:T(4,128)S(1)} fusion(f32[4]{0:T(128)} %constant.76.clone), kind=kLoop, calls=%fused_computation.16 | loop fusion | flops 16 | bytes 80 | tf_op jit(solution)/shard_map/mul | solution.py:45
  8.8 0.1 reshape.147
  9.0 0.7 %compare_select_fusion.1 = s32[64]{0:T(128)S(1)} fusion(s32[64]{0:T(128)} %param.9), kind=kLoop, calls=%fused_computation.14 | loop fusion | flops 192 | bytes 512 | tf_op jit(solution)/shard_map/select_n | solution.py:69
  9.6 0.8 %gather_fusion = s32[64]{0:T(128)S(1)} fusion(s32[96]{0:T(128)S(1)} %pad_add_fusion, s32[1024]{0:T(1024)S(1)} %pad_clamp_fusion.1), kind=kCustom, calls=%fused_computation | custom fusion | bytes 768 | tf_op jit(solution)/shard_map/gather | solution.py:69
  10.4 7.6 %collective-permute-done.1 = f32[64,4,640]{2,1,0:T(4,128)S(1)} collective-permute-done((f32[64,4,640]{2,1,0:T(4,128)}, f32[64,4,640]{2,1,0:T(4,128)S(1)}, u32[]{:S(2)}, u32[]{:S(2)}) %collective-permute-start.1) | collective-permute-done | bytes 655392 | tf_op jit(solution)/shard_map/ppermute | solution.py:21
  18.0 3.0 %collective-permute-done = f32[64,4,640]{2,1,0:T(4,128)} collective-permute-done((f32[64,4,640]{2,1,0:T(4,128)}, f32[64,4,640]{2,1,0:T(4,128)}, u32[]{:S(2)}, u32[]{:S(2)}) %collective-permute-start) | collective-permute-done | bytes 655392 | tf_op jit(solution)/shard_map/ppermute | solution.py:19
  21.1 1.5 %pad_maximum_fusion = f32[192,4,640]{2,1,0:T(4,128)S(1)} fusion(f32[64,4,640]{2,1,0:T(4,128)S(1)} %collective-permute-done.1, f32[64,4,640]{2,1,0:T(4,128)S(1)} %copy-done, f32[64,4,640]{2,1,0:T(4,128)} %collective-permute-done), kind=kLoop, calls=%fused_computation.2 | loop fusion | flops 983040 | bytes 3932160 | tf_op jit(solution)/shard_map/concatenate | solution.py:17
  22.6 1.0 %gather_fusion.1 = f32[64,4,640]{2,1,0:T(4,128)S(1)} fusion(f32[192,4,640]{2,1,0:T(4,128)S(1)} %pad_maximum_fusion, s32[1024]{0:T(1024)S(1)} %pad_clamp_fusion), kind=kCustom, calls=%fused_computation.1 | custom fusion | bytes 1310976 | tf_op jit(solution)/shard_map/gather | solution.py:69
  23.5 0.4 copy.21
  24.0 0.5 fusion.7
  24.5 1.1 %copy.22 = f32[64,160,16]{1,2,0:T(8,128)S(1)} copy(f32[64,160,16]{0,2,1:T(8,128)S(1)} %bitcast.26) | data formatting | bytes 1310720 | tf_op jit(solution)/shard_map/reshape | solution.py:54
  25.8 2.1 %fusion.8 = (f32[160,16]{0,1:T(8,128)S(1)}, f32[64,160,16]{1,2,0:T(8,128)S(1)}) fusion(f32[64,160]{1,0:T(8,128)S(1)} %copy.25, f32[64,160]{1,0:T(8,128)S(1)} %copy.24, f32[64,160,16]{1,2,0:T(8,128)S(1)} %copy.22, f32[64,16,16]{2,1,0:T(8,128)} %copy.23), kind=kOutput, calls=%fused_computation.32 | convolution fusion | flops 31946240 | bytes 1468416 | tf_op jit(solution)/shard_map/epn,ecn->ecp/dot_general | solution.py:55
  28.0 0.1 reduce_sum.14
  28.1 0.1 convolution_bitcast_fusion
  28.2 9.9 %psum.14 = f32[40]{0:T(128)S(1)} all-reduce(f32[40]{0:T(128)S(1)} %convolution_bitcast_fusion), channel_id=1, replica_groups=mesh['elem'=8,'lev'=4] {'lev'}, use_global_device_ids=true, to_apply=%region_4.0 | all-reduce | flops 40 | bytes 320 | tf_op jit(solution)/shard_map/psum | solution.py:74
  38.1 13.6 %psum.15 = f32[40]{0:T(128)S(1)} all-reduce(f32[40]{0:T(128)S(1)} %psum.14), channel_id=1, replica_groups=mesh['elem'=8,'lev'=4] {'elem'}, use_global_device_ids=true, to_apply=%region_5.6 | all-reduce | flops 40 | bytes 320 | tf_op jit(solution)/shard_map/psum | solution.py:75
  51.8 1.1 %copy.26 = f32[64,160,16]{0,2,1:T(8,128)S(1)} copy(f32[64,160,16]{1,2,0:T(8,128)S(1)} %get-tuple-element.10) | data formatting | bytes 1310720 | tf_op jit(solution)/shard_map/min | solution.py:58
  52.9 0.2 bitcast_multiply_fusion
  53.1 1.2 %copy.27 = f32[64,4,640]{2,1,0:T(4,128)} copy(f32[64,4,640]{0,2,1:T(8,128)S(1)} %bitcast_multiply_fusion) | data formatting | bytes 1310720 | tf_op jit(solution)/shard_map/mul | solution.py:78
  (20 shorter events, 0.6 us)
Async XLA Ops:
  0.0 21.1 %copy-start = (f32[64,4,640]{2,1,0:T(4,128)S(1)}, f32[64,4,640]{2,1,0:T(4,128)}, u32[]{:S(2)}) copy-start(f32[64,4,640]{2,1,0:T(4,128)} %param.6) | copy-start | bytes 1966084
  0.0 18.0 %collective-permute-start.1 = (f32[64,4,640]{2,1,0:T(4,128)}, f32[64,4,640]{2,1,0:T(4,128)S(1)}, u32[]{:S(2)}, u32[]{:S(2)}) collective-permute-start(f32[64,4,640]{2,1,0:T(4,128)} %param.6), channel_id=1, source_target_pairs={{4,0},{8,4},{12,8},{16,12},{20,16},{24,20},{28,24},{0,28},{5,1},{9... | collective-permute-start | bytes 1966088 | tf_op jit(solution)/shard_map/ppermute | solution.py:21
  4.5 16.5 %collective-permute-start = (f32[64,4,640]{2,1,0:T(4,128)}, f32[64,4,640]{2,1,0:T(4,128)}, u32[]{:S(2)}, u32[]{:S(2)}) collective-permute-start(f32[64,4,640]{2,1,0:T(4,128)} %param.6), channel_id=1, source_target_pairs={{0,4},{4,8},{8,12},{12,16},{16,20},{20,24},{24,28},{28,0},{1,5},{5... | collective-permute-start | bytes 1966088 | tf_op jit(solution)/shard_map/ppermute | solution.py:19
  25.6 26.1 %copy-start.1 = (f32[40]{0:T(128)S(1)}, f32[40]{0:T(128)}, u32[]{:S(2)}) copy-start(f32[40]{0:T(128)} %param.10) | copy-start | bytes 484
where the time goes:
time: 54.6 us; the launch traced here: 54.3 us
  blocking collectives  23.5 us (43%)
  waiting for transfers between devices  10.6 us (19%)
  local copies, waits for them, and re-layouts  7.18 us (13%)
  other arithmetic  4.66 us (9%)
  starting transfers between devices  4.52 us (8%)
  matrix products  3.75 us (7%)
    psum x1, blocking collectives, per_device(): global_mass = lax.psum(column_mass, 'elem')  13.6 us
    psum x1, blocking collectives, per_device(): column_mass = lax.psum(local_mass, 'lev')  9.89 us
    ppermute x1, waiting for transfers between devices, with_halo(): lax.ppermute(head, axis, [((i + 1) % count, i) for i in range(count)])  7.59 us
    ppermute x1, starting transfers between devices, with_halo(): lax.ppermute(head, axis, [((i + 1) % count, i) for i in range(count)])  4.52 us
    ppermute x1, waiting for transfers between devices, with_halo(): lax.ppermute(tail, axis, [(i, (i + 1) % count) for i in range(count)])  3.03 us
    gather x3, local copies, waits for them, and re-layouts, per_device(): source_rows = beside_all[slot_pos[source]]  2.17 us
    dot_general x1, matrix products, interpolate(): jnp.einsum('epn,ecn->ecp', matrix, values, precision=lax.Precision.HIGHEST)  2.15 us
    concatenate x1, other arithmetic, with_halo(): jnp.concatenate([lax.ppermute(tail, axis, [(i, (i + 1) % count) for i in...  1.51 us
  transfers between devices with their start and end apart: 2, of which 2 were waited for; matrix products, arithmetic and copies ran while one was open for 11% of the time, Pallas kernels for 0%

commit v1 on v0

v1 whole, which is shorter than its diff:
```python
import functools
import math

import jax
import jax.numpy as jnp
from jax import lax
from jax.experimental import pallas as pl
from jax.experimental.pallas import tpu as pltpu
from jax.sharding import PartitionSpec as P

NPTS = 16
SIDE = 8
LANES = 128
UNROLL = 4
MESH = pl.DeviceIdType.MESH
NODES = [-1.0, -math.sqrt(0.2), math.sqrt(0.2), 1.0]


def basis(x):
    d = [x - g for g in NODES]
    scale = [1.0 / math.prod(NODES[i] - NODES[k] for k in range(4) if k != i) for i in range(4)]
    low, high = d[0] * d[1], d[2] * d[3]
    parts = [d[1] * high, d[0] * high, low * d[3], low * d[2]]
    return [p * s for p, s in zip(parts, scale)]


def permute(v, index):
    return jnp.take_along_axis(v, index, axis=1, mode="promise_in_bounds")


def kernel(ne, nl, nelem, levels, chunks, slots, *refs):
    x_hbm, reft_ref, req_ref, src_ref, tm_ref, clip_out, fac_out = refs[:7]
    tabs = refs[7 : 7 + chunks]
    (sendb, halo, gbuf, clipb, rows, coef, massb, mrecv, req_r, req_l,
     in_sem, out_sem, rq_send, rq_recv, h_send, h_recv, m_send, m_recv, e_sem, l_sem) = refs[7 + chunks :]
    me_e, me_l = lax.axis_index("elem"), lax.axis_index("lev")
    right, left = lax.rem(me_e + 1, ne), lax.rem(me_e + ne - 1, ne)
    pairs = nelem // 2
    lrounds = [1 << j for j in range(int(math.log2(nl)))]
    erounds = [1 << j for j in range(int(math.log2(ne)) - 1)]

    loads = [pltpu.make_async_copy(x_hbm.at[:, c], tabs[c].at[pl.ds(0, nelem)], in_sem.at[c]) for c in range(chunks)]

    def hello(sem, e, l):
        pl.semaphore_signal(sem, inc=1, device_id=(e, l), device_id_type=MESH)

    barrier = pltpu.get_barrier_semaphore()
    hello(barrier, right, me_l)
    hello(barrier, left, me_l)
    for d in lrounds:
        hello(barrier, me_e, me_l ^ d)
    for load in loads:
        load.start()
    pl.semaphore_wait(barrier, 2 + len(lrounds))

    def remote(src, dst, ssem, rsem, e, l):
        return pltpu.make_async_remote_copy(
            src_ref=src, dst_ref=dst, send_sem=ssem, recv_sem=rsem, device_id=(e, l), device_id_type=MESH
        )

    ask_l = remote(req_ref, req_r, rq_send.at[0], rq_recv.at[0], left, me_l)
    ask_r = remote(req_ref, req_l, rq_send.at[1], rq_recv.at[1], right, me_l)
    ask_l.start()
    ask_r.start()

    steps = []
    for j, d in enumerate(erounds):
        fwd, back = lax.rem(me_e + d, ne), lax.rem(me_e + ne - d, ne)
        steps.append((lambda j=j, f=fwd, b=back: (hello(e_sem.at[j], f, me_l), hello(e_sem.at[j], b, me_l)),
                      lambda j=j: pl.semaphore_wait(e_sem.at[j], 2)))
    for j, d in enumerate(lrounds):
        steps.append((lambda j=j, d=d: hello(l_sem.at[j], me_e, me_l ^ d),
                      lambda j=j: pl.semaphore_wait(l_sem.at[j], 1)))
    steps[0][0]()

    lane = lax.broadcasted_iota(jnp.int32, (8, LANES), 1)
    point = lane % NPTS
    hi, lo = point // 4, point % 4

    spread = (lax.broadcasted_iota(jnp.int32, (NPTS, LANES), 1) % NPTS
              == lax.broadcasted_iota(jnp.int32, (NPTS, LANES), 0)).astype(jnp.float32)
    refs_f = reft_ref[...].astype(jnp.float32)
    tiled = lax.dot_general(refs_f, spread, (((0,), (0,)), ((), ())), preferred_element_type=jnp.float32)
    rep = (lax.broadcasted_iota(jnp.int32, (nelem * 4, nelem), 0) // 4
           == lax.broadcasted_iota(jnp.int32, (nelem * 4, nelem), 1)).astype(jnp.float32)
    rows[...] = jnp.dot(rep, tiled, preferred_element_type=jnp.float32)

    def shuffle(parts, which):
        return [jnp.where(which == 0, parts[k], jnp.where(which == 1, parts[1 ^ k],
                jnp.where(which == 2, parts[2 ^ k], parts[3 ^ k]))) for k in range(4)]

    def fill(i, carry):
        for u in range(UNROLL):
            q = i * UNROLL + u
            r = rows[pl.ds(pl.multiple_of(q * 8, 8), 8), :]
            a = jnp.floor((r + 0.5) * (1.0 / SIDE))
            b = r - SIDE * a
            la = shuffle(basis(-1.0 + a * (2.0 / (SIDE - 1))), hi)
            lb = shuffle(basis(-1.0 + b * (2.0 / (SIDE - 1))), lo)
            for k in range(NPTS):
                coef[k, q] = la[k // 4] * lb[k % 4]
        return carry

    lax.fori_loop(0, pairs // UNROLL, fill, 0)

    if len(steps) > 1:
        steps[0][1]()
        steps[1][0]()
    at = 1

    ask_l.wait()
    ask_r.wait()
    sends = []
    wanted = [[jnp.maximum(req_r[0, s], 0) for s in range(slots)], [jnp.maximum(req_l[1, s], 0) for s in range(slots)]]
    for c in range(chunks):
        loads[c].wait()
        for side, to in ((0, right), (1, left)):
            for s in range(slots):
                sendb[c, side, s] = tabs[c][wanted[side][s]]
            copy = remote(sendb.at[c, side], halo.at[c, side], h_send.at[c, side], h_recv.at[c, side], to, me_l)
            copy.start()
            sends.append(copy)

    while at < len(steps):
        steps[at][1]()
        if at + 1 < len(steps):
            steps[at + 1][0]()
        at += 1

    index = [lane ^ k for k in range(NPTS)]
    totals, stores = [], []
    for c in range(chunks):
        for side in range(2):
            sends[2 * c + side].wait_recv()
            tabs[c][pl.ds(nelem + side * slots, slots)] = halo[c, side]
        for q in range(pairs):
            gbuf[c, q, 0:4] = tabs[c][src_ref[2 * q]]
            gbuf[c, q, 4:8] = tabs[c][src_ref[2 * q + 1]]

        def work(i, acc, c=c):
            qs = [i * UNROLL + u for u in range(UNROLL)]
            vs = [gbuf[c, q] for q in qs]
            low, high, out = list(vs), list(vs), [coef[0, q] * v for q, v in zip(qs, vs)]
            for k in range(1, NPTS):
                for u in range(UNROLL):
                    w = permute(vs[u], index[k])
                    out[u] = out[u] + coef[k, qs[u]] * w
                    if k < 4:
                        low[u], high[u] = jnp.minimum(low[u], w), jnp.maximum(high[u], w)
            for k in (4, 8):
                for u in range(UNROLL):
                    low[u] = jnp.minimum(low[u], permute(low[u], index[k]))
                    high[u] = jnp.maximum(high[u], permute(high[u], index[k]))
            for u in range(UNROLL):
                res = jnp.minimum(jnp.maximum(out[u], low[u]), high[u])
                clipb[c, 2 * qs[u]] = res[0:4]
                clipb[c, 2 * qs[u] + 1] = res[4:8]
                acc = acc + res
            return acc

        totals.append(lax.fori_loop(0, pairs // UNROLL, work, jnp.zeros((8, LANES), jnp.float32)))
        store = pltpu.make_async_copy(clipb.at[c], clip_out.at[:, c], out_sem.at[c])
        store.start()
        stores.append(store)

    edge = [1.0 / 6.0, 5.0 / 6.0]
    weight = jnp.where((hi == 0) | (hi == 3), edge[0], edge[1]) * jnp.where((lo == 0) | (lo == 3), edge[0], edge[1])
    row = lax.broadcasted_iota(jnp.int32, (8, LANES), 0)
    part = jnp.zeros((8, LANES), jnp.float32)
    for c in range(chunks):
        one = jnp.sum(totals[c], axis=0, keepdims=True)
        part = jnp.where(row == c, one, part)
    part = part * weight
    for k in (1, 2, 4, 8):
        part = part + permute(part, index[k])
    packed = jnp.sum(jnp.where(point == row, part, 0.0), axis=0, keepdims=True)
    massb[0] = packed

    count = ne * nl

    def tell(de):
        e = lax.rem(me_e + de, ne)
        for dl in range(nl):
            l = lax.rem(me_l + dl, nl)
            slot = de * nl + dl - 1
            if isinstance(de, int) and slot < 0:
                continue
            remote(massb.at[0], mrecv.at[slot], m_send, m_recv, e, l).start()

    def tell_loop(de, carry):
        tell(de)
        return carry

    if count <= 64:
        for de in range(ne):
            tell(de)
    else:
        tell(0)
        lax.fori_loop(1, ne, tell_loop, 0)

    tm = jnp.zeros((8, LANES), jnp.float32)
    group = row * (LANES // NPTS) + lane // NPTS
    for t in range(chunks * LANES // NPTS):
        tm = jnp.where(group == t, tm_ref[t], tm)
    tm = tm * (4.0 * nelem * ne * levels * nl)
    for copy in sends:
        copy.wait_send()
    for store in stores:
        store.wait()
    everyone = remote(mrecv, mrecv, m_send, m_recv, right, me_l)
    everyone.wait_recv()
    mass = packed
    if count <= 64:
        for s in range(count - 1):
            mass = mass + mrecv[s]
    else:
        mass = lax.fori_loop(0, count - 1, lambda s, m: m + mrecv[s], mass)
    full = permute(jnp.broadcast_to(mass, (8, LANES)), (lane // NPTS) * NPTS + row)
    fac_out[...] = tm / full
    everyone.wait_send()


def per_device(ne, nl, tracers, ref_index, requests, source, target_mean):
    nelem, levels, width = tracers.shape
    chunks = width // LANES
    slots = requests.shape[2]
    x = tracers.reshape(nelem, levels, chunks, LANES).transpose(0, 2, 1, 3)
    f32 = jnp.float32
    vm = lambda *s: pltpu.VMEM(s, f32)
    dma = lambda *s: pltpu.SemaphoreType.DMA(s)
    smem, any_, vmem = (pl.BlockSpec(memory_space=m) for m in (pltpu.SMEM, pl.ANY, pltpu.VMEM))
    clipped, factor = pl.pallas_call(
        functools.partial(kernel, ne, nl, nelem, levels, chunks, slots),
        out_shape=(jax.ShapeDtypeStruct((nelem, chunks, levels, LANES), f32), jax.ShapeDtypeStruct((8, LANES), f32)),
        in_specs=[any_, vmem, smem, smem, smem],
        out_specs=(any_, vmem),
        scratch_shapes=[vm(nelem + 2 * slots, levels, LANES) for _ in range(chunks)] + [
            vm(chunks, 2, slots, levels, LANES),
            vm(chunks, 2, slots, levels, LANES),
            vm(chunks, nelem // 2, 8, LANES),
            vm(chunks, nelem, levels, LANES),
            vm(nelem * levels, LANES),
            vm(NPTS, nelem // 2, 8, LANES),
            vm(1, 1, LANES),
            vm(ne * nl - 1, 1, LANES),
            pltpu.SMEM((2, slots), jnp.int32),
            pltpu.SMEM((2, slots), jnp.int32),
            dma(chunks), dma(chunks), dma(2), dma(2), dma(chunks, 2), dma(chunks, 2),
            pltpu.SemaphoreType.DMA, pltpu.SemaphoreType.DMA,
            pltpu.SemaphoreType.REGULAR((max(int(math.log2(ne)) - 1, 1),)),
            pltpu.SemaphoreType.REGULAR((max(int(math.log2(nl)), 1),)),
        ],
        compiler_params=pltpu.CompilerParams(collective_id=0, has_side_effects=True),
    )(x, ref_index.T, requests[0], source, target_mean)
    out = clipped * factor[:chunks][None, :, None, :]
    return out.transpose(0, 2, 1, 3).reshape(nelem, levels, width)


def solution(mesh):
    placed = (P("elem", "lev", None), P("elem", None), P("elem", None, None), P("elem"), P())
    return jax.shard_map(
        functools.partial(per_device, mesh.shape["elem"], mesh.shape["lev"]),
        mesh=mesh, in_specs=placed, out_specs=P("elem", "lev", None), check_vma=False,
    )
```

time: 54.6 us -> 29.9 us (0.55)
  Pallas kernels: 0 us -> 27 us
  blocking collectives: 23.5 us -> 0 us
  waiting for transfers between devices: 10.6 us -> 0 us
  local copies, waits for them, and re-layouts: 7.18 us -> 0.66 us
  starting transfers between devices: 4.52 us -> 0 us
  matrix products: 3.75 us -> 0 us
  other arithmetic: 4.66 us -> 2.04 us
    pallas_call x0 -> x1, Pallas kernels: none -> 27 us  [per_device(): pl.pallas_call(functools.partial(kernel, ne, nl, nelem, levels, chunks, s...]
    psum x2 -> x0, blocking collectives: 23.5 us -> none  [the longest x1 13.6 us: per_device(): global_mass = lax.psum(column_mass, 'elem')]
    ppermute x2 -> x0, waiting for transfers between devices: 10.6 us -> none  [the longest x1 7.59 us: with_halo(): lax.ppermute(head, axis, [((i + 1) % count, i) for i in range(count)])]
    ppermute x2 -> x0, starting transfers between devices: 4.52 us -> none  [the longest x1 4.52 us: with_halo(): lax.ppermute(head, axis, [((i + 1) % count, i) for i in range(count)])]
    dot_general x3 -> x0, matrix products: 3.75 us -> none  [the longest x1 2.15 us: interpolate(): jnp.einsum('epn,ecn->ecp', matrix, values, precision=lax.Precision.HIGHEST)]
    gather x3 -> x0, local copies, waits for them, and re-layouts: 2.17 us -> none  [per_device(): source_rows = beside_all[slot_pos[source]]]
    reshape x0 -> x1, other arithmetic: none -> 2.04 us  [per_device(): return out.transpose(0, 2, 1, 3).reshape(nelem, levels, width)]
    concatenate x2 -> x0, other arithmetic: 1.59 us -> none  [the longest x1 1.51 us: with_halo(): jnp.concatenate([lax.ppermute(tail, axis, [(i, (i + 1) % count) for i in...]
  transfers between devices with their start and end apart: 2 -> 0, of which waited for: 2 -> 0; matrix products, arithmetic and copies ran while one was open for 11% -> 0% of each run, Pallas kernels for 0% -> 0%
where the time goes in v1:
time: 29.9 us; the launch traced here: 29.7 us
  Pallas kernels  27 us (90%)
  other arithmetic  2.04 us (7%)
  local copies, waits for them, and re-layouts  0.66 us (2%)
    pallas_call x1, Pallas kernels, per_device(): pl.pallas_call(functools.partial(kernel, ne, nl, nelem, levels, chunks, s...  27 us
    reshape x1, other arithmetic, per_device(): return out.transpose(0, 2, 1, 3).reshape(nelem, levels, width)  2.04 us
    unnamed x2, local copies, waits for them, and re-layouts  0.66 us

profile of v1, /device:TPU:0, one launch (start us, length us, event | category | flops | bytes accessed | tf_op | source)
XLA Modules:
  0.0 29.7 jit_solution(11634314094159242535)
XLA Ops:
  0.0 27.0 %shard_map.55 = (f32[64,5,4,128]{3,2,1,0:T(4,128)}, f32[8,128]{1,0:T(8,128)}) custom-call(f32[64,5,4,128]{3,2,1,0:T(4,128)} %bitcast.10, s32[16,64]{1,0:T(8,128)} %bitcast.11, s32[2,16]{1,0:T(2,128)} %bitcast.13, s32[64]{0:T(128)} %refs_3_.1, f32[40]{0:T(128)} %refs_4_.1), custom_call_target="tpu_custom_call" | custom-call | tf_op jit(solution)/shard_map/pallas_call | solution.py:232
  27.0 0.0 copy-start
  27.0 0.7 %copy-done = f32[8,128]{1,0:T(8,128)S(1)} copy-done((f32[8,128]{1,0:T(8,128)S(1)}, f32[8,128]{1,0:T(8,128)}, u32[]{:S(2)}) %copy-start) | copy-done | bytes 4120
  27.7 2.0 %multiply_bitcast_fusion = f32[64,4,640]{2,1,0:T(4,128)} fusion(f32[64,5,4,128]{3,2,1,0:T(4,128)} %get-tuple-element.7, f32[5,128]{1,0:T(8,128)S(1)} %bitcast.12), kind=kLoop, calls=%fused_computation | loop fusion | flops 163840 | bytes 1313280 | tf_op jit(solution)/shard_map/reshape | solution.py:256
Async XLA Ops:
  27.0 0.7 %copy-start = (f32[8,128]{1,0:T(8,128)S(1)}, f32[8,128]{1,0:T(8,128)}, u32[]{:S(2)}) copy-start(f32[8,128]{1,0:T(8,128)} %get-tuple-element.8) | copy-start | bytes 12292

commit v2 on v1

--- a/solution.py
+++ b/solution.py
@@ -11,7 +11,6 @@
 NPTS = 16
 SIDE = 8
 LANES = 128
-UNROLL = 4
 MESH = pl.DeviceIdType.MESH
 NODES = [-1.0, -math.sqrt(0.2), math.sqrt(0.2), 1.0]
 
@@ -30,16 +29,16 @@
 
 def kernel(ne, nl, nelem, levels, chunks, slots, *refs):
     x_hbm, reft_ref, req_ref, src_ref, tm_ref, clip_out, fac_out = refs[:7]
-    tabs = refs[7 : 7 + chunks]
-    (sendb, halo, gbuf, clipb, rows, coef, massb, mrecv, req_r, req_l,
-     in_sem, out_sem, rq_send, rq_recv, h_send, h_recv, m_send, m_recv, e_sem, l_sem) = refs[7 + chunks :]
+    (tab, sendb, halo, gbuf, turned, clipb, coef, massb, mrecv, req_r, req_l,
+     in_sem, out_sem, rq_send, rq_recv, h_send, h_recv, m_send, m_recv, e_sem, l_sem) = refs[7:]
     me_e, me_l = lax.axis_index("elem"), lax.axis_index("lev")
     right, left = lax.rem(me_e + 1, ne), lax.rem(me_e + ne - 1, ne)
-    pairs = nelem // 2
+    halves = nelem * levels // LANES
+    each = nelem // halves
     lrounds = [1 << j for j in range(int(math.log2(nl)))]
     erounds = [1 << j for j in range(int(math.log2(ne)) - 1)]
 
-    loads = [pltpu.make_async_copy(x_hbm.at[:, c], tabs[c].at[pl.ds(0, nelem)], in_sem.at[c]) for c in range(chunks)]
+    loads = [pltpu.make_async_copy(x_hbm.at[:, c], tab.at[c, pl.ds(0, nelem)], in_sem.at[c]) for c in range(chunks)]
 
     def hello(sem, e, l):
         pl.semaphore_signal(sem, inc=1, device_id=(e, l), device_id_type=MESH)
@@ -77,31 +76,18 @@
     point = lane % NPTS
     hi, lo = point // 4, point % 4
 
-    spread = (lax.broadcasted_iota(jnp.int32, (NPTS, LANES), 1) % NPTS
-              == lax.broadcasted_iota(jnp.int32, (NPTS, LANES), 0)).astype(jnp.float32)
     refs_f = reft_ref[...].astype(jnp.float32)
-    tiled = lax.dot_general(refs_f, spread, (((0,), (0,)), ((), ())), preferred_element_type=jnp.float32)
-    rep = (lax.broadcasted_iota(jnp.int32, (nelem * 4, nelem), 0) // 4
-           == lax.broadcasted_iota(jnp.int32, (nelem * 4, nelem), 1)).astype(jnp.float32)
-    rows[...] = jnp.dot(rep, tiled, preferred_element_type=jnp.float32)
-
-    def shuffle(parts, which):
-        return [jnp.where(which == 0, parts[k], jnp.where(which == 1, parts[1 ^ k],
-                jnp.where(which == 2, parts[2 ^ k], parts[3 ^ k]))) for k in range(4)]
-
-    def fill(i, carry):
-        for u in range(UNROLL):
-            q = i * UNROLL + u
-            r = rows[pl.ds(pl.multiple_of(q * 8, 8), 8), :]
-            a = jnp.floor((r + 0.5) * (1.0 / SIDE))
-            b = r - SIDE * a
-            la = shuffle(basis(-1.0 + a * (2.0 / (SIDE - 1))), hi)
-            lb = shuffle(basis(-1.0 + b * (2.0 / (SIDE - 1))), lo)
-            for k in range(NPTS):
-                coef[k, q] = la[k // 4] * lb[k % 4]
-        return carry
-
-    lax.fori_loop(0, pairs // UNROLL, fill, 0)
+    rep = (lax.broadcasted_iota(jnp.int32, (nelem, nelem * levels), 1) // levels
+           == lax.broadcasted_iota(jnp.int32, (nelem, nelem * levels), 0)).astype(jnp.float32)
+    spread = jnp.dot(refs_f, rep, preferred_element_type=jnp.float32)
+    for h in range(halves):
+        r = spread[:, h * LANES : (h + 1) * LANES]
+        a = jnp.floor((r + 0.5) * (1.0 / SIDE))
+        b = r - SIDE * a
+        la = basis(-1.0 + a * (2.0 / (SIDE - 1)))
+        lb = basis(-1.0 + b * (2.0 / (SIDE - 1)))
+        for n in range(NPTS):
+            coef[h, n] = la[n // 4] * lb[n % 4]
 
     if len(steps) > 1:
         steps[0][1]()
@@ -110,16 +96,19 @@
 
     ask_l.wait()
     ask_r.wait()
-    sends = []
+    for load in loads:
+        load.wait()
     wanted = [[jnp.maximum(req_r[0, s], 0) for s in range(slots)], [jnp.maximum(req_l[1, s], 0) for s in range(slots)]]
+
+    def rows_to(c, side):
+        to = left if side else right
+        return remote(sendb.at[c, side], halo.at[c, side], h_send.at[c, side], h_recv.at[c, side], to, me_l)
+
     for c in range(chunks):
-        loads[c].wait()
-        for side, to in ((0, right), (1, left)):
+        for side in range(2):
             for s in range(slots):
-                sendb[c, side, s] = tabs[c][wanted[side][s]]
-            copy = remote(sendb.at[c, side], halo.at[c, side], h_send.at[c, side], h_recv.at[c, side], to, me_l)
-            copy.start()
-            sends.append(copy)
+                sendb[c, side, s] = tab[c, wanted[side][s]]
+            rows_to(c, side).start()
 
     while at < len(steps):
         steps[at][1]()
@@ -128,48 +117,36 @@
         at += 1
 
     index = [lane ^ k for k in range(NPTS)]
-    totals, stores = [], []
-    for c in range(chunks):
+    row = lax.broadcasted_iota(jnp.int32, (8, LANES), 0)
+    store = lambda c: pltpu.make_async_copy(clipb.at[c], clip_out.at[:, c], out_sem.at[c])
+
+    def work(c, part):
         for side in range(2):
-            sends[2 * c + side].wait_recv()
-            tabs[c][pl.ds(nelem + side * slots, slots)] = halo[c, side]
-        for q in range(pairs):
-            gbuf[c, q, 0:4] = tabs[c][src_ref[2 * q]]
-            gbuf[c, q, 4:8] = tabs[c][src_ref[2 * q + 1]]
-
-        def work(i, acc, c=c):
-            qs = [i * UNROLL + u for u in range(UNROLL)]
-            vs = [gbuf[c, q] for q in qs]
-            low, high, out = list(vs), list(vs), [coef[0, q] * v for q, v in zip(qs, vs)]
-            for k in range(1, NPTS):
-                for u in range(UNROLL):
-                    w = permute(vs[u], index[k])
-                    out[u] = out[u] + coef[k, qs[u]] * w
-                    if k < 4:
-                        low[u], high[u] = jnp.minimum(low[u], w), jnp.maximum(high[u], w)
-            for k in (4, 8):
-                for u in range(UNROLL):
-                    low[u] = jnp.minimum(low[u], permute(low[u], index[k]))
-                    high[u] = jnp.maximum(high[u], permute(high[u], index[k]))
-            for u in range(UNROLL):
-                res = jnp.minimum(jnp.maximum(out[u], low[u]), high[u])
-                clipb[c, 2 * qs[u]] = res[0:4]
-                clipb[c, 2 * qs[u] + 1] = res[4:8]
-                acc = acc + res
-            return acc
-
-        totals.append(lax.fori_loop(0, pairs // UNROLL, work, jnp.zeros((8, LANES), jnp.float32)))
-        store = pltpu.make_async_copy(clipb.at[c], clip_out.at[:, c], out_sem.at[c])
-        store.start()
-        stores.append(store)
+            rows_to(c, side).wait_recv()
+            tab[c, pl.ds(nelem + side * slots, slots)] = halo[c, side]
+        total = jnp.zeros((LANES, LANES), jnp.float32)
+        for h in range(halves):
+            for q in range(each):
+                gbuf[h, q * levels : (q + 1) * levels] = tab[c, src_ref[h * each + q]]
+            turned[h] = gbuf[h].T
+            done = []
+            for t in range(LANES // NPTS):
+                v = turned[h, t * NPTS : (t + 1) * NPTS]
+                low, high = jnp.min(v, axis=0, keepdims=True), jnp.max(v, axis=0, keepdims=True)
+                out = jnp.zeros((NPTS, LANES), jnp.float32)
+                for n in range(NPTS):
+                    out = out + coef[h, n] * turned[h, t * NPTS + n : t * NPTS + n + 1]
+                done.append(jnp.minimum(jnp.maximum(out, low), high))
+            back = jnp.concatenate(done, axis=0).T
+            clipb[c, h * each : (h + 1) * each] = back.reshape(each, levels, LANES)
+            total = total + back
+        store(c).start()
+        return jnp.where(row == c, jnp.sum(total, axis=0, keepdims=True), part)
+
+    part = lax.fori_loop(0, chunks, work, jnp.zeros((8, LANES), jnp.float32))
 
     edge = [1.0 / 6.0, 5.0 / 6.0]
     weight = jnp.where((hi == 0) | (hi == 3), edge[0], edge[1]) * jnp.where((lo == 0) | (lo == 3), edge[0], edge[1])
-    row = lax.broadcasted_iota(jnp.int32, (8, LANES), 0)
-    part = jnp.zeros((8, LANES), jnp.float32)
-    for c in range(chunks):
-        one = jnp.sum(totals[c], axis=0, keepdims=True)
-        part = jnp.where(row == c, one, part)
     part = part * weight
     for k in (1, 2, 4, 8):
         part = part + permute(part, index[k])
@@ -203,10 +180,10 @@
     for t in range(chunks * LANES // NPTS):
         tm = jnp.where(group == t, tm_ref[t], tm)
     tm = tm * (4.0 * nelem * ne * levels * nl)
-    for copy in sends:
-        copy.wait_send()
-    for store in stores:
-        store.wait()
+    for c in range(chunks):
+        for side in range(2):
+            rows_to(c, side).wait_send()
+        store(c).wait()
     everyone = remote(mrecv, mrecv, m_send, m_recv, right, me_l)
     everyone.wait_recv()
     mass = packed
@@ -234,13 +211,14 @@
         out_shape=(jax.ShapeDtypeStruct((nelem, chunks, levels, LANES), f32), jax.ShapeDtypeStruct((8, LANES), f32)),
         in_specs=[any_, vmem, smem, smem, smem],
         out_specs=(any_, vmem),
-        scratch_shapes=[vm(nelem + 2 * slots, levels, LANES) for _ in range(chunks)] + [
+        scratch_shapes=[
+            vm(chunks, nelem + 2 * slots, levels, LANES),
             vm(chunks, 2, slots, levels, LANES),
             vm(chunks, 2, slots, levels, LANES),
-            vm(chunks, nelem // 2, 8, LANES),
+            vm(nelem * levels // LANES, LANES, LANES),
+            vm(nelem * levels // LANES, LANES, LANES),
             vm(chunks, nelem, levels, LANES),
-            vm(nelem * levels, LANES),
-            vm(NPTS, nelem // 2, 8, LANES),
+            vm(nelem * levels // LANES, NPTS, NPTS, LANES),
             vm(1, 1, LANES),
             vm(ne * nl - 1, 1, LANES),
             pltpu.SMEM((2, slots), jnp.int32),

time: 29.9 us -> 22.8 us (0.76)
  Pallas kernels: 27 us -> 19.9 us
    pallas_call x1, Pallas kernels: 27 us -> 19.9 us  [per_device(): pl.pallas_call(functools.partial(kernel, ne, nl, nelem, levels, chunks, s...]
where the time goes in v2:
time: 22.8 us; the launch traced here: 22.6 us
  Pallas kernels  19.9 us (87%)
  other arithmetic  2.04 us (9%)
  local copies, waits for them, and re-layouts  0.66 us (3%)
    pallas_call x1, Pallas kernels, per_device(): pl.pallas_call(functools.partial(kernel, ne, nl, nelem, levels, chunks, s...  19.9 us
    reshape x1, other arithmetic, per_device(): return out.transpose(0, 2, 1, 3).reshape(nelem, levels, width)  2.04 us
    unnamed x2, local copies, waits for them, and re-layouts  0.66 us

profile of v2, /device:TPU:0, one launch (start us, length us, event | category | flops | bytes accessed | tf_op | source)
XLA Modules:
  0.0 22.6 jit_solution(18210034279605897197)
XLA Ops:
  0.0 19.9 %shard_map.55 = (f32[64,5,4,128]{3,2,1,0:T(4,128)}, f32[8,128]{1,0:T(8,128)}) custom-call(f32[64,5,4,128]{3,2,1,0:T(4,128)} %bitcast.10, s32[16,64]{1,0:T(8,128)} %bitcast.11, s32[2,16]{1,0:T(2,128)} %bitcast.13, s32[64]{0:T(128)} %refs_3_.1, f32[40]{0:T(128)} %refs_4_.1), custom_call_target="tpu_custom_call" | custom-call | tf_op jit(solution)/shard_map/pallas_call | solution.py:209
  19.9 0.0 copy-start
  19.9 0.7 %copy-done = f32[8,128]{1,0:T(8,128)S(1)} copy-done((f32[8,128]{1,0:T(8,128)S(1)}, f32[8,128]{1,0:T(8,128)}, u32[]{:S(2)}) %copy-start) | copy-done | bytes 4120
  20.5 2.0 %multiply_bitcast_fusion = f32[64,4,640]{2,1,0:T(4,128)} fusion(f32[64,5,4,128]{3,2,1,0:T(4,128)} %get-tuple-element.7, f32[5,128]{1,0:T(8,128)S(1)} %bitcast.12), kind=kLoop, calls=%fused_computation | loop fusion | flops 163840 | bytes 1313280 | tf_op jit(solution)/shard_map/reshape | solution.py:234
Async XLA Ops:
  19.9 0.7 %copy-start = (f32[8,128]{1,0:T(8,128)S(1)}, f32[8,128]{1,0:T(8,128)}, u32[]{:S(2)}) copy-start(f32[8,128]{1,0:T(8,128)} %get-tuple-element.8) | copy-start | bytes 12292

commit v3 on v2

--- a/solution.py
+++ b/solution.py
@@ -28,9 +28,9 @@
 
 
 def kernel(ne, nl, nelem, levels, chunks, slots, *refs):
-    x_hbm, reft_ref, req_ref, src_ref, tm_ref, clip_out, fac_out = refs[:7]
-    (tab, sendb, halo, gbuf, turned, clipb, coef, massb, mrecv, req_r, req_l,
-     in_sem, out_sem, rq_send, rq_recv, h_send, h_recv, m_send, m_recv, e_sem, l_sem) = refs[7:]
+    x_hbm, reft_hbm, req_hbm, src_hbm, tm_hbm, clip_out, fac_out = refs[:7]
+    (reft_ref, req_ref, src_ref, tm_ref, tab, sendb, halo, gbuf, turned, coef, massb, mrecv, req_r, req_l,
+     in_sem, small, rq_send, rq_recv, h_send, h_recv, m_send, m_recv, e_sem, l_sem) = refs[7:]
     me_e, me_l = lax.axis_index("elem"), lax.axis_index("lev")
     right, left = lax.rem(me_e + 1, ne), lax.rem(me_e + ne - 1, ne)
     halves = nelem * levels // LANES
@@ -40,6 +40,9 @@
 
     loads = [pltpu.make_async_copy(x_hbm.at[:, c], tab.at[c, pl.ds(0, nelem)], in_sem.at[c]) for c in range(chunks)]
 
+    fetch = [pltpu.make_async_copy(a, b, small.at[i]) for i, (a, b) in enumerate(
+        [(req_hbm, req_ref), (reft_hbm, reft_ref), (src_hbm, src_ref), (tm_hbm, tm_ref)])]
+
     def hello(sem, e, l):
         pl.semaphore_signal(sem, inc=1, device_id=(e, l), device_id_type=MESH)
 
@@ -48,8 +51,9 @@
     hello(barrier, left, me_l)
     for d in lrounds:
         hello(barrier, me_e, me_l ^ d)
-    for load in loads:
-        load.start()
+    for copy in fetch + loads:
+        copy.start()
+    fetch[0].wait()
     pl.semaphore_wait(barrier, 2 + len(lrounds))
 
     def remote(src, dst, ssem, rsem, e, l):
@@ -76,6 +80,7 @@
     point = lane % NPTS
     hi, lo = point // 4, point % 4
 
+    fetch[1].wait()
     refs_f = reft_ref[...].astype(jnp.float32)
     rep = (lax.broadcasted_iota(jnp.int32, (nelem, nelem * levels), 1) // levels
            == lax.broadcasted_iota(jnp.int32, (nelem, nelem * levels), 0)).astype(jnp.float32)
@@ -94,6 +99,8 @@
         steps[1][0]()
     at = 1
 
+    fetch[2].wait()
+    fetch[3].wait()
     ask_l.wait()
     ask_r.wait()
     for load in loads:
@@ -118,7 +125,6 @@
 
     index = [lane ^ k for k in range(NPTS)]
     row = lax.broadcasted_iota(jnp.int32, (8, LANES), 0)
-    store = lambda c: pltpu.make_async_copy(clipb.at[c], clip_out.at[:, c], out_sem.at[c])
 
     def work(c, part):
         for side in range(2):
@@ -138,9 +144,8 @@
                     out = out + coef[h, n] * turned[h, t * NPTS + n : t * NPTS + n + 1]
                 done.append(jnp.minimum(jnp.maximum(out, low), high))
             back = jnp.concatenate(done, axis=0).T
-            clipb[c, h * each : (h + 1) * each] = back.reshape(each, levels, LANES)
+            clip_out[h * each : (h + 1) * each, c] = back.reshape(each, levels, LANES)
             total = total + back
-        store(c).start()
         return jnp.where(row == c, jnp.sum(total, axis=0, keepdims=True), part)
 
     part = lax.fori_loop(0, chunks, work, jnp.zeros((8, LANES), jnp.float32))
@@ -183,7 +188,6 @@
     for c in range(chunks):
         for side in range(2):
             rows_to(c, side).wait_send()
-        store(c).wait()
     everyone = remote(mrecv, mrecv, m_send, m_recv, right, me_l)
     everyone.wait_recv()
     mass = packed
@@ -205,30 +209,33 @@
     f32 = jnp.float32
     vm = lambda *s: pltpu.VMEM(s, f32)
     dma = lambda *s: pltpu.SemaphoreType.DMA(s)
-    smem, any_, vmem = (pl.BlockSpec(memory_space=m) for m in (pltpu.SMEM, pl.ANY, pltpu.VMEM))
+    hbm, vmem = (pl.BlockSpec(memory_space=m) for m in (pltpu.HBM, pltpu.VMEM))
     clipped, factor = pl.pallas_call(
         functools.partial(kernel, ne, nl, nelem, levels, chunks, slots),
         out_shape=(jax.ShapeDtypeStruct((nelem, chunks, levels, LANES), f32), jax.ShapeDtypeStruct((8, LANES), f32)),
-        in_specs=[any_, vmem, smem, smem, smem],
-        out_specs=(any_, vmem),
+        in_specs=[hbm] * 5,
+        out_specs=(vmem, vmem),
         scratch_shapes=[
+            pltpu.VMEM((NPTS, nelem), jnp.int32),
+            pltpu.SMEM((2, slots), jnp.int32),
+            pltpu.SMEM((nelem,), jnp.int32),
+            pltpu.SMEM((chunks * LANES // NPTS,), f32),
             vm(chunks, nelem + 2 * slots, levels, LANES),
             vm(chunks, 2, slots, levels, LANES),
             vm(chunks, 2, slots, levels, LANES),
             vm(nelem * levels // LANES, LANES, LANES),
             vm(nelem * levels // LANES, LANES, LANES),
-            vm(chunks, nelem, levels, LANES),
             vm(nelem * levels // LANES, NPTS, NPTS, LANES),
             vm(1, 1, LANES),
             vm(ne * nl - 1, 1, LANES),
             pltpu.SMEM((2, slots), jnp.int32),
             pltpu.SMEM((2, slots), jnp.int32),
-            dma(chunks), dma(chunks), dma(2), dma(2), dma(chunks, 2), dma(chunks, 2),
+            dma(chunks), dma(4), dma(2), dma(2), dma(chunks, 2), dma(chunks, 2),
             pltpu.SemaphoreType.DMA, pltpu.SemaphoreType.DMA,
             pltpu.SemaphoreType.REGULAR((max(int(math.log2(ne)) - 1, 1),)),
             pltpu.SemaphoreType.REGULAR((max(int(math.log2(nl)), 1),)),
         ],
-        compiler_params=pltpu.CompilerParams(collective_id=0, has_side_effects=True),
+        compiler_params=pltpu.CompilerParams(collective_id=0, has_side_effects=True, vmem_limit_bytes=8 * 2**20),
     )(x, ref_index.T, requests[0], source, target_mean)
     out = clipped * factor[:chunks][None, :, None, :]
     return out.transpose(0, 2, 1, 3).reshape(nelem, levels, width)

time: 22.8 us -> 22.1 us (0.969)
  local copies, waits for them, and re-layouts: 0.66 us -> 2.48 us
  Pallas kernels: 19.9 us -> 18.4 us
  other arithmetic: 2.04 us -> 0.95 us
    unnamed x2 -> x10, local copies, waits for them, and re-layouts: 0.66 us -> 2.48 us
    pallas_call x1, Pallas kernels: 19.9 us -> 18.4 us  [per_device(): pl.pallas_call(functools.partial(kernel, ne, nl, nelem, levels, chunks, s...]
    reshape x1, other arithmetic: 2.04 us -> 0.95 us  [per_device(): return out.transpose(0, 2, 1, 3).reshape(nelem, levels, width)]
where the time goes in v3:
time: 22.1 us; the launch traced here: 21.9 us
  Pallas kernels  18.4 us (83%)
  local copies, waits for them, and re-layouts  2.48 us (11%)
  other arithmetic  0.95 us (4%)
    pallas_call x1, Pallas kernels, per_device(): pl.pallas_call(functools.partial(kernel, ne, nl, nelem, levels, chunks, s...  18.4 us
    unnamed x10, local copies, waits for them, and re-layouts  2.48 us
    reshape x1, other arithmetic, per_device(): return out.transpose(0, 2, 1, 3).reshape(nelem, levels, width)  0.95 us

profile of v3, /device:TPU:0, one launch (start us, length us, event | category | flops | bytes accessed | tf_op | source)
XLA Modules:
  0.0 21.9 jit_solution(4420792244593698791)
XLA Ops:
  0.0 0.0 copy-start.4
  0.0 0.0 copy-start.2
  0.0 0.0 copy-start.3
  0.0 0.6 %copy-done.4 = f32[40]{0:T(128)S(1)} copy-done((f32[40]{0:T(128)S(1)}, f32[40]{0:T(128)}, u32[]{:S(2)}) %copy-start.4) | copy-done | bytes 184
  0.7 0.0 copy-done.2
  0.7 0.0 copy-done.3
  0.7 0.0 copy-start
  0.7 1.1 %copy-done = f32[64,4,640]{2,1,0:T(4,128)S(1)} copy-done((f32[64,4,640]{2,1,0:T(4,128)S(1)}, f32[64,4,640]{2,1,0:T(4,128)}, u32[]{:S(2)}) %copy-start) | copy-done | bytes 655384
  1.8 0.0 copy-start.1
  1.8 0.7 %copy-done.1 = s32[64,16]{0,1:T(8,128)S(1)} copy-done((s32[64,16]{0,1:T(8,128)S(1)}, s32[64,16]{0,1:T(8,128)}, u32[]{:S(2)}) %copy-start.1) | copy-done | bytes 4120
  2.5 18.4 %shard_map.55 = (f32[64,5,4,128]{3,2,1,0:T(4,128)S(1)}, f32[8,128]{1,0:T(8,128)S(1)}) custom-call(f32[64,5,4,128]{3,2,1,0:T(4,128)S(1)} %bitcast.10, s32[16,64]{1,0:T(8,128)S(1)} %bitcast.11, s32[2,16]{1,0:T(2,128)S(1)} %bitcast.13, s32[64]{0:T(128)S(1)} %copy-done.3, f32[40]{0:T(128)S(1)} %copy-done.4), custom_call_target="tpu_custom_call" | custom-call | tf_op jit(solution)/shard_map/pallas_call | solution.py:213
  20.9 1.0 %multiply_bitcast_fusion = f32[64,4,640]{2,1,0:T(4,128)} fusion(f32[64,5,4,128]{3,2,1,0:T(4,128)S(1)} %get-tuple-element.7, f32[5,128]{1,0:T(8,128)S(1)} %bitcast.12), kind=kLoop, calls=%fused_computation | loop fusion | flops 163840 | bytes 1313280 | tf_op jit(solution)/shard_map/reshape | solution.py:241
Async XLA Ops:
  0.0 0.7 %copy-start.4 = (f32[40]{0:T(128)S(1)}, f32[40]{0:T(128)}, u32[]{:S(2)}) copy-start(f32[40]{0:T(128)} %refs_4_.1) | copy-start | bytes 484
  0.0 0.7 %copy-start.2 = (s32[1,2,16]{2,1,0:T(2,128)S(1)}, s32[1,2,16]{2,1,0:T(2,128)}, u32[]{:S(2)}) copy-start(s32[1,2,16]{2,1,0:T(2,128)} %param.7) | copy-start | bytes 388
  0.0 0.7 %copy-start.3 = (s32[64]{0:T(128)S(1)}, s32[64]{0:T(128)}, u32[]{:S(2)}) copy-start(s32[64]{0:T(128)} %refs_3_.1) | copy-start | bytes 772
  0.7 1.1 %copy-start = (f32[64,4,640]{2,1,0:T(4,128)S(1)}, f32[64,4,640]{2,1,0:T(4,128)}, u32[]{:S(2)}) copy-start(f32[64,4,640]{2,1,0:T(4,128)} %param.5) | copy-start | bytes 1966084
  1.8 0.7 %copy-start.1 = (s32[64,16]{0,1:T(8,128)S(1)}, s32[64,16]{0,1:T(8,128)}, u32[]{:S(2)}) copy-start(s32[64,16]{0,1:T(8,128)} %param.6) | copy-start | bytes 12292

commit v4 on v3

--- a/solution.py
+++ b/solution.py
@@ -117,10 +117,9 @@
                 sendb[c, side, s] = tab[c, wanted[side][s]]
             rows_to(c, side).start()
 
-    while at < len(steps):
+    while at < len(steps) - 2:
         steps[at][1]()
-        if at + 1 < len(steps):
-            steps[at + 1][0]()
+        steps[at + 1][0]()
         at += 1
 
     index = [lane ^ k for k in range(NPTS)]
@@ -146,12 +145,19 @@
             back = jnp.concatenate(done, axis=0).T
             clip_out[h * each : (h + 1) * each, c] = back.reshape(each, levels, LANES)
             total = total + back
+
+        @pl.when(c == 0)
+        def _():
+            steps[-2][1]()
+            steps[-1][0]()
+
         return jnp.where(row == c, jnp.sum(total, axis=0, keepdims=True), part)
 
     part = lax.fori_loop(0, chunks, work, jnp.zeros((8, LANES), jnp.float32))
 
     edge = [1.0 / 6.0, 5.0 / 6.0]
     weight = jnp.where((hi == 0) | (hi == 3), edge[0], edge[1]) * jnp.where((lo == 0) | (lo == 3), edge[0], edge[1])
+    steps[-1][1]()
     part = part * weight
     for k in (1, 2, 4, 8):
         part = part + permute(part, index[k])
@@ -235,7 +241,7 @@
             pltpu.SemaphoreType.REGULAR((max(int(math.log2(ne)) - 1, 1),)),
             pltpu.SemaphoreType.REGULAR((max(int(math.log2(nl)), 1),)),
         ],
-        compiler_params=pltpu.CompilerParams(collective_id=0, has_side_effects=True, vmem_limit_bytes=8 * 2**20),
+        compiler_params=pltpu.CompilerParams(collective_id=0, has_side_effects=True, vmem_limit_bytes=55_600_000),
     )(x, ref_index.T, requests[0], source, target_mean)
     out = clipped * factor[:chunks][None, :, None, :]
     return out.transpose(0, 2, 1, 3).reshape(nelem, levels, width)

time: 22.1 us -> 21.1 us (0.955)
  local copies, waits for them, and re-layouts: 2.48 us -> 1.39 us
    unnamed x10 -> x8, local copies, waits for them, and re-layouts: 2.48 us -> 1.39 us
where the time goes in v4:
time: 21.1 us; the launch traced here: 20.8 us
  Pallas kernels  18.5 us (88%)
  local copies, waits for them, and re-layouts  1.39 us (7%)
  other arithmetic  0.95 us (5%)
    pallas_call x1, Pallas kernels, per_device(): pl.pallas_call(functools.partial(kernel, ne, nl, nelem, levels, chunks, s...  18.5 us
    unnamed x8, local copies, waits for them, and re-layouts  1.39 us
    reshape x1, other arithmetic, per_device(): return out.transpose(0, 2, 1, 3).reshape(nelem, levels, width)  0.95 us

profile of v4, /device:TPU:0, one launch (start us, length us, event | category | flops | bytes accessed | tf_op | source)
XLA Modules:
  0.0 20.8 jit_solution(8675640357033353374)
XLA Ops:
  0.0 0.0 copy-start.3
  0.0 0.0 copy-start.1
  0.0 0.0 copy-start.2
  0.0 0.6 %copy-done.3 = f32[40]{0:T(128)S(1)} copy-done((f32[40]{0:T(128)S(1)}, f32[40]{0:T(128)}, u32[]{:S(2)}) %copy-start.3) | copy-done | bytes 184
  0.7 0.0 copy-done.1
  0.7 0.0 copy-done.2
  0.7 0.0 copy-start
  0.7 0.7 %copy-done = s32[64,16]{0,1:T(8,128)S(1)} copy-done((s32[64,16]{0,1:T(8,128)S(1)}, s32[64,16]{0,1:T(8,128)}, u32[]{:S(2)}) %copy-start) | copy-done | bytes 4120
  1.4 18.5 %shard_map.55 = (f32[64,5,4,128]{3,2,1,0:T(4,128)S(1)}, f32[8,128]{1,0:T(8,128)S(1)}) custom-call(f32[64,5,4,128]{3,2,1,0:T(4,128)} %bitcast.13, s32[16,64]{1,0:T(8,128)S(1)} %bitcast.10, s32[2,16]{1,0:T(2,128)S(1)} %bitcast.12, s32[64]{0:T(128)S(1)} %copy-done.2, f32[40]{0:T(128)S(1)} %copy-done.3), custom_call_target="tpu_custom_call" | custom-call | tf_op jit(solution)/shard_map/pallas_call | solution.py:219
  19.9 1.0 %multiply_bitcast_fusion = f32[64,4,640]{2,1,0:T(4,128)} fusion(f32[64,5,4,128]{3,2,1,0:T(4,128)S(1)} %get-tuple-element.7, f32[5,128]{1,0:T(8,128)S(1)} %bitcast.11), kind=kLoop, calls=%fused_computation | loop fusion | flops 163840 | bytes 1313280 | tf_op jit(solution)/shard_map/reshape | solution.py:247
Async XLA Ops:
  0.0 0.7 %copy-start.3 = (f32[40]{0:T(128)S(1)}, f32[40]{0:T(128)}, u32[]{:S(2)}) copy-start(f32[40]{0:T(128)} %refs_4_.1) | copy-start | bytes 484
  0.0 0.7 %copy-start.1 = (s32[1,2,16]{2,1,0:T(2,128)S(1)}, s32[1,2,16]{2,1,0:T(2,128)}, u32[]{:S(2)}) copy-start(s32[1,2,16]{2,1,0:T(2,128)} %param.7) | copy-start | bytes 388
  0.0 0.7 %copy-start.2 = (s32[64]{0:T(128)S(1)}, s32[64]{0:T(128)}, u32[]{:S(2)}) copy-start(s32[64]{0:T(128)} %refs_3_.1) | copy-start | bytes 772
  0.7 0.7 %copy-start = (s32[64,16]{0,1:T(8,128)S(1)}, s32[64,16]{0,1:T(8,128)}, u32[]{:S(2)}) copy-start(s32[64,16]{0,1:T(8,128)} %param.6) | copy-start | bytes 12292

commit v5 on v4

--- a/solution.py
+++ b/solution.py
@@ -168,7 +168,7 @@
 
     def tell(de):
         e = lax.rem(me_e + de, ne)
-        for dl in range(nl):
+        for dl in reversed(range(nl)):
             l = lax.rem(me_l + dl, nl)
             slot = de * nl + dl - 1
             if isinstance(de, int) and slot < 0:
@@ -180,7 +180,7 @@
         return carry
 
     if count <= 64:
-        for de in range(ne):
+        for de in sorted(range(ne), key=lambda d: -min(d, ne - d)):
             tell(de)
     else:
         tell(0)

time: 21.1 us -> 21.2 us (level)
  no operation moved by 1% of the time
where the time goes in v5:
time: 21.2 us; the launch traced here: 21 us
  Pallas kernels  18.6 us (88%)
  local copies, waits for them, and re-layouts  1.39 us (7%)
  other arithmetic  0.95 us (4%)
    pallas_call x1, Pallas kernels, per_device(): pl.pallas_call(functools.partial(kernel, ne, nl, nelem, levels, chunks, s...  18.6 us
    unnamed x8, local copies, waits for them, and re-layouts  1.39 us
    reshape x1, other arithmetic, per_device(): return out.transpose(0, 2, 1, 3).reshape(nelem, levels, width)  0.95 us

profile of v5, /device:TPU:0, one launch (start us, length us, event | category | flops | bytes accessed | tf_op | source)
XLA Modules:
  0.0 21.0 jit_solution(9088736239389855529)
XLA Ops:
  0.0 0.0 copy-start.3
  0.0 0.0 copy-start.1
  0.0 0.0 copy-start.2
  0.0 0.6 %copy-done.3 = f32[40]{0:T(128)S(1)} copy-done((f32[40]{0:T(128)S(1)}, f32[40]{0:T(128)}, u32[]{:S(2)}) %copy-start.3) | copy-done | bytes 184
  0.7 0.0 copy-done.1
  0.7 0.0 copy-done.2
  0.7 0.0 copy-start
  0.7 0.7 %copy-done = s32[64,16]{0,1:T(8,128)S(1)} copy-done((s32[64,16]{0,1:T(8,128)S(1)}, s32[64,16]{0,1:T(8,128)}, u32[]{:S(2)}) %copy-start) | copy-done | bytes 4120
  1.4 18.6 %shard_map.55 = (f32[64,5,4,128]{3,2,1,0:T(4,128)S(1)}, f32[8,128]{1,0:T(8,128)S(1)}) custom-call(f32[64,5,4,128]{3,2,1,0:T(4,128)} %bitcast.13, s32[16,64]{1,0:T(8,128)S(1)} %bitcast.10, s32[2,16]{1,0:T(2,128)S(1)} %bitcast.12, s32[64]{0:T(128)S(1)} %copy-done.2, f32[40]{0:T(128)S(1)} %copy-done.3), custom_call_target="tpu_custom_call" | custom-call | tf_op jit(solution)/shard_map/pallas_call | solution.py:219
  20.0 1.0 %multiply_bitcast_fusion = f32[64,4,640]{2,1,0:T(4,128)} fusion(f32[64,5,4,128]{3,2,1,0:T(4,128)S(1)} %get-tuple-element.7, f32[5,128]{1,0:T(8,128)S(1)} %bitcast.11), kind=kLoop, calls=%fused_computation | loop fusion | flops 163840 | bytes 1313280 | tf_op jit(solution)/shard_map/reshape | solution.py:247
Async XLA Ops:
  0.0 0.7 %copy-start.3 = (f32[40]{0:T(128)S(1)}, f32[40]{0:T(128)}, u32[]{:S(2)}) copy-start(f32[40]{0:T(128)} %refs_4_.1) | copy-start | bytes 484
  0.0 0.7 %copy-start.1 = (s32[1,2,16]{2,1,0:T(2,128)S(1)}, s32[1,2,16]{2,1,0:T(2,128)}, u32[]{:S(2)}) copy-start(s32[1,2,16]{2,1,0:T(2,128)} %param.7) | copy-start | bytes 388
  0.0 0.7 %copy-start.2 = (s32[64]{0:T(128)S(1)}, s32[64]{0:T(128)}, u32[]{:S(2)}) copy-start(s32[64]{0:T(128)} %refs_3_.1) | copy-start | bytes 772
  0.7 0.7 %copy-start = (s32[64,16]{0,1:T(8,128)S(1)}, s32[64,16]{0,1:T(8,128)}, u32[]{:S(2)}) copy-start(s32[64,16]{0,1:T(8,128)} %param.6) | copy-start | bytes 12292
